TPU v7x, 32 devices: a whole 2x2x4 slice. The times are simulated.
32 devices in a mesh: grp: 2 (over x), row: 16 (over z, y, core).
Axes of the slice: x: 2, y: 2, z: 4, core: 2. Of those that a mesh axis runs over, the one named last changes fastest.
Arguments:
- tiles: bfloat16 [192, 512, 512], P(('grp', 'row')), may hold values from -0.15625 to 0.15625
- tile_row: int32 [192], P(('grp', 'row')), may hold values from 0 to 63, as said below
- tile_col: int32 [192], P(('grp', 'row')), may hold values from 0 to 63, as said below
- tile_count: int32 [32], P(('grp', 'row')), may hold values from 3 to 6, as said below
- q_block: bfloat16 [32768, 256], P(('grp', 'row')), may hold values from -80 to 80
Outputs:
- q_next: float32 [32768, 256], P(('grp', 'row'))
Inputs may be any that keep to these rules, and one draw needn't show every extreme that they name: `tile_row`: each slot names one of its device's tile rows: d * 2 to d * 2 + 1 for device d. `tile_col`: each slot's tile column is (tile_row + o) mod 64 with o from minus 2 to 2; no two slots of one device name the same pair of tile row and tile column. `tile_count`: some device has all 6 slots live.
All inputs are finite; a program needn't handle non-finite values.
Results may differ from a plain program's by a relative error of at most 0.0029.
Values may be sent and summed in bfloat16 or wider, within the bound.
A program may use at most 64 MiB of HBM per device.

v0:
```python
import jax
import jax.numpy as jnp
from jax import lax
from jax.sharding import PartitionSpec as P

H = 2


def padded_2(block, sides, width):
    for axis, dim in sides:
        count = lax.axis_size(axis)
        forward = [(i, i + 1) for i in range(count - 1)]
        forward.append((count - 1, 0))
        backward = [(target, source) for source, target in forward]
        low = lax.ppermute(
            lax.slice_in_dim(block, block.shape[dim] - width, None, axis=dim), axis, forward
        )
        high = lax.ppermute(lax.slice_in_dim(block, 0, width, axis=dim), axis, backward)
        block = jnp.concatenate([low, block, high], axis=dim)
    return block


def passed_along(block, axis, distance):
    devices = range(lax.axis_size(axis))
    route = [((i - distance) % len(devices), i) for i in devices]
    return lax.ppermute(block, axis, route)


def on_device(tiles, tile_row, tile_col, tile_count, q_block):
    slot_count, tile_size, unused_size = tiles.shape
    basis_width = q_block.shape[1]
    own_tiles = q_block.shape[0] // tile_size
    window = own_tiles + 2 * H
    tile_total = own_tiles * lax.axis_size("grp") * lax.axis_size("row")
    local_row = tile_row % own_tiles
    local_col = (tile_col - tile_row + H) % tile_total + local_row
    padded = padded_2(q_block, ((("grp", "row"), 0),), H * tile_size)
    stack = padded.reshape(window, tile_size, basis_width)
    live_slot = jnp.arange(slot_count, dtype=jnp.int32) < tile_count[0]
    blocks = stack[local_col]
    blocks = jnp.where(live_slot[:, None, None], blocks, jnp.zeros_like(blocks))
    products = jnp.einsum("sab,sbk->sak", tiles, blocks, preferred_element_type=jnp.float32)
    row_ids = jnp.arange(own_tiles, dtype=jnp.int32)
    row_place = ((local_row[None, :] == row_ids[:, None]) & live_slot[None, :]).astype(jnp.float32)
    aq_tiles = jnp.einsum(
        "rs,sak->rak", row_place, products, precision=lax.Precision.HIGHEST
    ).astype(jnp.bfloat16)
    row_part = aq_tiles[local_row]
    images = jnp.einsum("sab,sak->sbk", tiles, row_part, preferred_element_type=jnp.float32)
    column_ids = jnp.arange(window, dtype=jnp.int32)
    col_place = ((local_col[None, :] == column_ids[:, None]) & live_slot[None, :]).astype(
        jnp.float32
    )
    sums = jnp.einsum("cs,sbk->cbk", col_place, images, precision=lax.Precision.HIGHEST)
    own_part = sums[H : H + own_tiles]
    lower = sums[:H].astype(jnp.bfloat16).reshape(H * tile_size, basis_width)
    upper = sums[H + own_tiles :].astype(jnp.bfloat16).reshape(H * tile_size, basis_width)
    from_below = passed_along(upper, ("grp", "row"), 1)
    from_above = passed_along(lower, ("grp", "row"), -1)
    below_tiles = from_below.astype(jnp.float32).reshape(H, tile_size, basis_width)
    above_tiles = from_above.astype(jnp.float32).reshape(H, tile_size, basis_width)
    own_part = own_part + below_tiles
    own_part = own_part + above_tiles
    local_y = own_part.reshape(own_tiles * tile_size, basis_width)
    rows_total = tile_total * tile_size
    local_gram = jnp.dot(
        local_y.T, local_y, precision=lax.Precision.HIGHEST, preferred_element_type=jnp.float32
    )
    gram_matrix = lax.psum(local_gram, ("grp", "row")) / rows_total
    factor_low = jnp.linalg.cholesky(gram_matrix)
    return lax.linalg.triangular_solve(
        factor_low, local_y, left_side=False, lower=True, transpose_a=True
    )


def solution(mesh):
    placed = (
        P(("grp", "row"), None, None),
        P(("grp", "row")),
        P(("grp", "row")),
        P(("grp", "row")),
        P(("grp", "row"), None),
    )
    return jax.shard_map(
        on_device, mesh=mesh, in_specs=placed, out_specs=P(("grp", "row"), None), check_vma=False
    )
```

profile of v0, /device:TPU:0, one launch (start us, length us, event | category | flops | bytes accessed | tf_op | source)
XLA Modules:
  0.0 289.4 jit_solution(1188874127921917125)
XLA Ops:
  7.0 5.9 %collective-permute-start.1 = (bf16[1024,256]{1,0:T(8,128)(2,1)}, bf16[1024,256]{1,0:T(8,128)(2,1)S(1)}, u32[]{:S(2)}, u32[]{:S(2)}) collective-permute-start(bf16[1024,256]{1,0:T(8,128)(2,1)} %param.9), channel_id=1, source_target_pairs={{1,0},{2,1},{3,2},{4,3},{5,4},{6,5},{7,6},{8,7},{9,8},{10,9},{11,1... | collective-permute-start | bytes 1572872 | tf_op jit(solution)/shard_map/ppermute | solution.py:18
  15.0 5.1 %collective-permute-done = bf16[1024,256]{1,0:T(8,128)(2,1)S(1)} collective-permute-done((bf16[1024,256]{1,0:T(8,128)(2,1)}, bf16[1024,256]{1,0:T(8,128)(2,1)S(1)}, u32[]{:S(2)}, u32[]{:S(2)}) %collective-permute-start) | collective-permute-done | bytes 524320 | tf_op jit(solution)/shard_map/ppermute | solution.py:15
  20.1 2.3 pad_maximum_fusion
  22.4 3.3 %gather_fusion = bf16[6,512,256]{2,1,0:T(8,128)(2,1)} fusion(bf16[6,512,256]{2,1,0:T(8,128)(2,1)} %bitcast.63, s32[1024]{0:T(1024)S(1)} %pad_clamp_fusion.1), kind=kCustom, calls=%fused_computation | custom fusion | bytes 3145752 | tf_op jit(solution)/shard_map/gather | solution.py:40
  25.7 4.3 %convolution_bitcast_fusion.1 = f32[6,512,256]{1,2,0:T(8,128)} fusion(bf16[6,512,512]{2,1,0:T(8,128)(2,1)S(1)} %copy-done, bf16[6,512,256]{2,1,0:T(8,128)(2,1)} %gather_fusion, pred[6]{0:T(512)(128)(4,1)S(1)} %iota_compare_fusion.4), kind=kOutput, calls=%fused_computation.5 | convolution fusion | flops 806092800 | bytes 7864326 | tf_op jit(solution)/shard_map/sab,sbk->sak/dot_general | solution.py:42
  29.9 5.1 %copy.32 = f32[6,512,256]{2,0,1:T(8,128)} copy(f32[6,512,256]{1,2,0:T(8,128)} %convolution_bitcast_fusion.1) | data formatting | bytes 6291456 | tf_op jit(solution)/shard_map/sab,sbk->sak/dot_general | solution.py:42
  35.1 4.3 %convolution_convert_fusion = bf16[2,512,256]{2,0,1:T(2,128)(2,1)S(1)} fusion(f32[6,512,256]{2,0,1:T(8,128)} %copy.32, pred[6]{0:T(512)(128)(4,1)S(1)} %iota_compare_fusion.4, s32[6]{0:T(128)S(1)} %get-tuple-element.22), kind=kOutput, calls=%fused_computation.9 | convolution fusion | flops 19136536 | bytes 3670046 | tf_op jit(solution)/shard_map/rs,sak->rak/dot_general | solution.py:45
  40.2 2.9 gather_fusion.1
  43.1 4.1 %convolution_bitcast_fusion = f32[6,512,256]{1,2,0:T(8,128)} fusion(bf16[6,512,256]{2,1,0:T(8,128)(2,1)} %gather_fusion.1, bf16[6,512,512]{2,1,0:T(8,128)(2,1)S(1)} %copy-done), kind=kOutput, calls=%fused_computation.4 | convolution fusion | flops 805306368 | bytes 7864320 | tf_op jit(solution)/shard_map/sab,sak->sbk/dot_general | solution.py:49
  47.2 5.1 %copy.35 = f32[6,512,256]{2,0,1:T(8,128)} copy(f32[6,512,256]{1,2,0:T(8,128)} %convolution_bitcast_fusion) | data formatting | bytes 6291456 | tf_op jit(solution)/shard_map/sab,sak->sbk/dot_general | solution.py:49
  52.3 4.3 %fusion.32 = (bf16[6,512,256]{2,0,1:T(8,128)(2,1)S(1)}, f32[6,512,256]{2,0,1:T(8,128)S(1)}) fusion(f32[6,512,256]{2,0,1:T(8,128)} %copy.35, s32[6]{0:T(128)S(1)} %get-tuple-element.24, pred[6]{0:T(512)(128)(4,1)S(1)} %iota_compare_fusion.4), kind=kOutput, calls=%fused_computation.71 | convolution fusion | flops 57409608 | bytes 7864350 | tf_op jit(solution)/shard_map/cs,sbk->cbk/dot_general | solution.py:54
  57.5 4.0 %collective-permute-start.2 = (bf16[1024,256]{1,0:T(8,128)(2,1)S(1)}, bf16[1024,256]{1,0:T(8,128)(2,1)S(1)}, u32[]{:S(2)}, u32[]{:S(2)}) collective-permute-start(bf16[1024,256]{1,0:T(8,128)(2,1)S(1)} %bitcast.64), channel_id=1, source_target_pairs={{31,0},{0,1},{1,2},{2,3},{3,4},{4,5},{5,6},{6,7},{7,8},{8,9},{9,10... | collective-permute-start | bytes 1572872 | tf_op jit(solution)/shard_map/ppermute | solution.py:26
  61.6 1.6 collective-permute-start.3
  63.7 6.1 %collective-permute-done.2 = bf16[1024,256]{1,0:T(8,128)(2,1)S(1)} collective-permute-done((bf16[1024,256]{1,0:T(8,128)(2,1)S(1)}, bf16[1024,256]{1,0:T(8,128)(2,1)S(1)}, u32[]{:S(2)}, u32[]{:S(2)}) %collective-permute-start.2) | collective-permute-done | bytes 524320 | tf_op jit(solution)/shard_map/ppermute | solution.py:26
  71.0 2.5 convolution_bitcast_fusion.2
  73.6 132.1 %all-reduce.3.cloned.1.call-done = f32[256,256]{0,1:T(8,128)} async-done(((f32[256,256]{0,1:T(8,128)}), f32[256,256]{0,1:T(8,128)}) %all-reduce.3.cloned.1.call-update) | async-done | bytes 262160 | tf_op jit(solution)/shard_map/psum | solution.py:69
  205.6 1.7 broadcast_multiply_fusion
  207.3 1.1 copy.41
  210.1 11.7 %cholesky.50 = f32[128,128]{1,0:T(8,128)S(1)} custom-call(f32[128,128]{1,0:T(8,128)S(1)} %cholesky.118), custom_call_target="Cholesky" | custom-call | tf_op jit(solution)/shard_map/jit(cholesky)/cholesky | solution.py:70
  221.9 9.8 %custom-call.14 = f32[1,128,128]{1,2,0:T(8,128)S(1)} custom-call(f32[1,128,128]{2,1,0:T(8,128)S(1)} %get-tuple-element.32), custom_call_target="InvertDiagBlocksLowerTriangular" | custom-call | tf_op jit(solution)/shard_map/jit(cholesky)/cholesky | solution.py:70
  231.7 1.0 constant_dynamic-update-slice_fusion.1
  232.7 1.1 convolution_subtract_fusion
  233.8 11.9 %cholesky.105 = f32[128,128]{1,0:T(8,128)S(1)} custom-call(f32[128,128]{1,0:T(8,128)S(1)} %convolution_subtract_fusion), custom_call_target="Cholesky" | custom-call | tf_op jit(solution)/shard_map/jit(cholesky)/cholesky | solution.py:70
  248.8 5.3 %while.1 = (s32[]{:T(128)}, f32[256,256]{1,0:T(8,128)S(1)}, s32[2,2]{1,0:T(2,128)S(1)}, f32[2,128,128]{2,1,0:T(8,128)}, s32[]{:T(128)}) while((s32[]{:T(128)}, f32[256,256]{1,0:T(8,128)S(1)}, s32[2,2]{1,0:T(2,128)S(1)}, f32[2,128,128]{2,1,0:T(8,128)}, s32[]{:T(128)}) %tuple.27), condition=%wide.while_cond, body=%wide.while_body.sunk | while | flops 2 | bytes 132705 | solution.py:71
  249.5 2.0 bitcast_dynamic-update-slice_fusion.2
  252.2 2.0 bitcast_dynamic-update-slice_fusion.2
  254.1 20.5 %custom-call.15 = f32[2,128,128]{1,2,0:T(8,128)S(1)} custom-call(f32[2,128,128]{2,1,0:T(8,128)} %get-tuple-element.12), custom_call_target="InvertDiagBlocksLowerTriangular" | custom-call | tf_op jit(solution)/shard_map/triangular_solve | solution.py:71
  274.6 1.7 fusion.5
  276.3 1.0 fusion.8
  277.3 1.7 fusion.4
  279.0 1.0 pad_maximum_fusion.1
  280.0 2.5 copy.42
  (38 shorter events, 10.2 us)
Async XLA Ops:
  6.5 19.2 %copy-start = (bf16[6,512,512]{2,1,0:T(8,128)(2,1)S(1)}, bf16[6,512,512]{2,1,0:T(8,128)(2,1)}, u32[]{:S(2)}) copy-start(bf16[6,512,512]{2,1,0:T(8,128)(2,1)} %param.5) | copy-start | bytes 9437188
  6.5 199.1 %all-reduce.3.cloned.1.call-start = ((), (), s32[]{:S(2)}) async-start(), calls=%async_computation | async-start | bytes 524288 | tf_op jit(solution)/shard_map/psum | solution.py:69
  6.5 13.6 %collective-permute-start = (bf16[1024,256]{1,0:T(8,128)(2,1)}, bf16[1024,256]{1,0:T(8,128)(2,1)S(1)}, u32[]{:S(2)}, u32[]{:S(2)}) collective-permute-start(bf16[1024,256]{1,0:T(8,128)(2,1)} %param.9), channel_id=1, source_target_pairs={{0,1},{1,2},{2,3},{3,4},{4,5},{5,6},{6,7},{7,8},{8,9},{9,10},{10,1... | collective-permute-start | bytes 1572872 | tf_op jit(solution)/shard_map/ppermute | solution.py:15
  7.0 13.1 %collective-permute-start.1 = (bf16[1024,256]{1,0:T(8,128)(2,1)}, bf16[1024,256]{1,0:T(8,128)(2,1)S(1)}, u32[]{:S(2)}, u32[]{:S(2)}) collective-permute-start(bf16[1024,256]{1,0:T(8,128)(2,1)} %param.9), channel_id=1, source_target_pairs={{1,0},{2,1},{3,2},{4,3},{5,4},{6,5},{7,6},{8,7},{9,8},{10,9},{11,1... | collective-permute-start | bytes 1572872 | tf_op jit(solution)/shard_map/ppermute | solution.py:18
  57.5 12.4 %collective-permute-start.2 = (bf16[1024,256]{1,0:T(8,128)(2,1)S(1)}, bf16[1024,256]{1,0:T(8,128)(2,1)S(1)}, u32[]{:S(2)}, u32[]{:S(2)}) collective-permute-start(bf16[1024,256]{1,0:T(8,128)(2,1)S(1)} %bitcast.64), channel_id=1, source_target_pairs={{31,0},{0,1},{1,2},{2,3},{3,4},{4,5},{5,6},{6,7},{7,8},{8,9},{9,10... | collective-permute-start | bytes 1572872 | tf_op jit(solution)/shard_map/ppermute | solution.py:26
  61.6 8.3 %collective-permute-start.3 = (bf16[1024,256]{1,0:T(8,128)(2,1)S(1)}, bf16[1024,256]{1,0:T(8,128)(2,1)S(1)}, u32[]{:S(2)}, u32[]{:S(2)}) collective-permute-start(bf16[1024,256]{1,0:T(8,128)(2,1)S(1)} %bitcast.65), channel_id=1, source_target_pairs={{1,0},{2,1},{3,2},{4,3},{5,4},{6,5},{7,6},{8,7},{9,8},{10,9},{11,1... | collective-permute-start | bytes 1572872 | tf_op jit(solution)/shard_map/ppermute | solution.py:26
  70.0 1.0 copy-start.1
  209.4 0.7 copy-start.3
  245.8 2.0 copy-start.2
Sparse Core Ops, SparseCore 0:
  73.7 131.9 all-reduce.2
where the time goes:
time: 290 us; the launch traced here: 289 us
  waiting for transfers between devices  143 us (49%)
  other arithmetic  63.2 us (22%)
  local copies, waits for them, and re-layouts  29.3 us (10%)
  matrix products  26 us (9%)
  between operations  15.5 us (5%)
  starting transfers between devices  12 us (4%)
    psum x1, waiting for transfers between devices, on_device(): gram_matrix = lax.psum(local_gram, ('grp', 'row')) / rows_total  132 us
    another operation x6, other arithmetic, on_device(): factor_low = jnp.linalg.cholesky(gram_matrix)  34.2 us
    another operation x4, other arithmetic, on_device(): lax.linalg.triangular_solve(factor_low, local_y, left_side=False, lower=T...  22.5 us
    ppermute x2, waiting for transfers between devices, passed_along(): return lax.ppermute(block, axis, route)  6.15 us
    ppermute x1, starting transfers between devices, padded_2(): lax.ppermute(lax.slice_in_dim(block, 0, width, axis=dim), axis, backward)  5.91 us
  transfers between devices with their start and end apart: 5, of which 4 were waited for; matrix products, arithmetic and copies ran while one was open for 1% of the time, Pallas kernels for 0%

commit v1 on v0

--- a/solution.py
+++ b/solution.py
@@ -4,6 +4,11 @@
 from jax.sharding import PartitionSpec as P
 
 H = 2
+
+
+def summed_here(shard, mesh_axis):
+    terms = lax.all_gather(shard, mesh_axis)
+    return jnp.sum(terms, axis=0)
 
 
 def padded_2(block, sides, width):
@@ -66,7 +71,7 @@
     local_gram = jnp.dot(
         local_y.T, local_y, precision=lax.Precision.HIGHEST, preferred_element_type=jnp.float32
     )
-    gram_matrix = lax.psum(local_gram, ("grp", "row")) / rows_total
+    gram_matrix = summed_here(local_gram, ("grp", "row")) / rows_total
     factor_low = jnp.linalg.cholesky(gram_matrix)
     return lax.linalg.triangular_solve(
         factor_low, local_y, left_side=False, lower=True, transpose_a=True

time: 290 us -> 243 us (0.84)
  waiting for transfers between devices: 143 us -> 94 us
    psum x1 -> x0, waiting for transfers between devices: 132 us -> none  [on_device(): gram_matrix = lax.psum(local_gram, ('grp', 'row')) / rows_total]
    all_gather x0 -> x1, waiting for transfers between devices: none -> 82.6 us  [summed_here(): terms = lax.all_gather(shard, mesh_axis)]
    reduce_sum x0 -> x1, other arithmetic: none -> 3.93 us  [summed_here(): return jnp.sum(terms, axis=0)]
where the time goes in v1:
time: 243 us; the launch traced here: 242 us
  waiting for transfers between devices  94 us (39%)
  other arithmetic  65.5 us (27%)
  local copies, waits for them, and re-layouts  29.1 us (12%)
  matrix products  26 us (11%)
  between operations  15.5 us (6%)
  starting transfers between devices  12 us (5%)
    all_gather x1, waiting for transfers between devices, summed_here(): terms = lax.all_gather(shard, mesh_axis)  82.6 us
    another operation x6, other arithmetic, on_device(): factor_low = jnp.linalg.cholesky(gram_matrix)  34.2 us
    another operation x4, other arithmetic, on_device(): lax.linalg.triangular_solve(factor_low, local_y, left_side=False, lower=T...  22.5 us
    ppermute x2, waiting for transfers between devices, passed_along(): return lax.ppermute(block, axis, route)  6.15 us
    ppermute x1, starting transfers between devices, padded_2(): lax.ppermute(lax.slice_in_dim(block, 0, width, axis=dim), axis, backward)  5.91 us
    ppermute x2, starting transfers between devices, passed_along(): return lax.ppermute(block, axis, route)  5.64 us
    another operation x6, local copies, waits for them, and re-layouts  5.28 us
    ppermute x1, waiting for transfers between devices, padded_2(): lax.ppermute(lax.slice_in_dim(block, block.shape[dim] - width, None, axis...  5.14 us
  transfers between devices with their start and end apart: 5, of which 4 were waited for; matrix products, arithmetic and copies ran while one was open for 1% of the time, Pallas kernels for 0%

profile of v1, /device:TPU:0, one launch (start us, length us, event | category | flops | bytes accessed | tf_op | source)
XLA Modules:
  0.0 242.0 jit_solution(8694359249189334284)
XLA Ops:
  7.0 5.9 %collective-permute-start.1 = (bf16[1024,256]{1,0:T(8,128)(2,1)}, bf16[1024,256]{1,0:T(8,128)(2,1)S(1)}, u32[]{:S(2)}, u32[]{:S(2)}) collective-permute-start(bf16[1024,256]{1,0:T(8,128)(2,1)} %param.9), channel_id=1, source_target_pairs={{1,0},{2,1},{3,2},{4,3},{5,4},{6,5},{7,6},{8,7},{9,8},{10,9},{11,1... | collective-permute-start | bytes 1572872 | tf_op jit(solution)/shard_map/ppermute | solution.py:23
  15.0 5.1 %collective-permute-done = bf16[1024,256]{1,0:T(8,128)(2,1)S(1)} collective-permute-done((bf16[1024,256]{1,0:T(8,128)(2,1)}, bf16[1024,256]{1,0:T(8,128)(2,1)S(1)}, u32[]{:S(2)}, u32[]{:S(2)}) %collective-permute-start) | collective-permute-done | bytes 524320 | tf_op jit(solution)/shard_map/ppermute | solution.py:20
  20.1 2.3 pad_maximum_fusion
  22.4 3.3 %gather_fusion = bf16[6,512,256]{2,1,0:T(8,128)(2,1)} fusion(bf16[6,512,256]{2,1,0:T(8,128)(2,1)} %bitcast.65, s32[1024]{0:T(1024)S(1)} %pad_clamp_fusion.1), kind=kCustom, calls=%fused_computation | custom fusion | bytes 3145752 | tf_op jit(solution)/shard_map/gather | solution.py:45
  25.7 4.3 %convolution_bitcast_fusion.1 = f32[6,512,256]{1,2,0:T(8,128)} fusion(bf16[6,512,512]{2,1,0:T(8,128)(2,1)S(1)} %copy-done, bf16[6,512,256]{2,1,0:T(8,128)(2,1)} %gather_fusion, pred[6]{0:T(512)(128)(4,1)S(1)} %iota_compare_fusion.4), kind=kOutput, calls=%fused_computation.5 | convolution fusion | flops 806092800 | bytes 7864326 | tf_op jit(solution)/shard_map/sab,sbk->sak/dot_general | solution.py:47
  29.9 5.1 %copy.46 = f32[6,512,256]{2,0,1:T(8,128)} copy(f32[6,512,256]{1,2,0:T(8,128)} %convolution_bitcast_fusion.1) | data formatting | bytes 6291456 | tf_op jit(solution)/shard_map/sab,sbk->sak/dot_general | solution.py:47
  35.1 4.3 %convolution_convert_fusion = bf16[2,512,256]{2,0,1:T(2,128)(2,1)S(1)} fusion(f32[6,512,256]{2,0,1:T(8,128)} %copy.46, pred[6]{0:T(512)(128)(4,1)S(1)} %iota_compare_fusion.4, s32[6]{0:T(128)S(1)} %get-tuple-element.22), kind=kOutput, calls=%fused_computation.9 | convolution fusion | flops 19136536 | bytes 3670046 | tf_op jit(solution)/shard_map/rs,sak->rak/dot_general | solution.py:50
  40.2 2.9 %gather_fusion.1 = bf16[6,512,256]{2,1,0:T(8,128)(2,1)} fusion(bf16[2,512,256]{2,1,0:T(8,128)(2,1)} %copy.47, s32[1024]{0:T(1024)S(1)} %pad_clamp_fusion), kind=kCustom, calls=%fused_computation.1 | custom fusion | bytes 3145752 | tf_op jit(solution)/shard_map/gather | solution.py:53
  43.1 4.1 %convolution_bitcast_fusion = f32[6,512,256]{1,2,0:T(8,128)} fusion(bf16[6,512,256]{2,1,0:T(8,128)(2,1)} %gather_fusion.1, bf16[6,512,512]{2,1,0:T(8,128)(2,1)S(1)} %copy-done), kind=kOutput, calls=%fused_computation.4 | convolution fusion | flops 805306368 | bytes 7864320 | tf_op jit(solution)/shard_map/sab,sak->sbk/dot_general | solution.py:54
  47.2 5.1 %copy.49 = f32[6,512,256]{2,0,1:T(8,128)} copy(f32[6,512,256]{1,2,0:T(8,128)} %convolution_bitcast_fusion) | data formatting | bytes 6291456 | tf_op jit(solution)/shard_map/sab,sak->sbk/dot_general | solution.py:54
  52.3 4.3 %fusion.32 = (bf16[6,512,256]{2,0,1:T(8,128)(2,1)S(1)}, f32[6,512,256]{2,0,1:T(8,128)S(1)}) fusion(f32[6,512,256]{2,0,1:T(8,128)} %copy.49, s32[6]{0:T(128)S(1)} %get-tuple-element.24, pred[6]{0:T(512)(128)(4,1)S(1)} %iota_compare_fusion.4), kind=kOutput, calls=%fused_computation.70 | convolution fusion | flops 57409608 | bytes 7864350 | tf_op jit(solution)/shard_map/cs,sbk->cbk/dot_general | solution.py:59
  57.5 4.0 %collective-permute-start.2 = (bf16[1024,256]{1,0:T(8,128)(2,1)S(1)}, bf16[1024,256]{1,0:T(8,128)(2,1)S(1)}, u32[]{:S(2)}, u32[]{:S(2)}) collective-permute-start(bf16[1024,256]{1,0:T(8,128)(2,1)S(1)} %bitcast.66), channel_id=1, source_target_pairs={{31,0},{0,1},{1,2},{2,3},{3,4},{4,5},{5,6},{6,7},{7,8},{8,9},{9,10... | collective-permute-start | bytes 1572872 | tf_op jit(solution)/shard_map/ppermute | solution.py:31
  61.6 1.6 collective-permute-start.3
  63.7 6.1 %collective-permute-done.2 = bf16[1024,256]{1,0:T(8,128)(2,1)S(1)} collective-permute-done((bf16[1024,256]{1,0:T(8,128)(2,1)S(1)}, bf16[1024,256]{1,0:T(8,128)(2,1)S(1)}, u32[]{:S(2)}, u32[]{:S(2)}) %collective-permute-start.2) | collective-permute-done | bytes 524320 | tf_op jit(solution)/shard_map/ppermute | solution.py:31
  71.0 2.6 %convolution_bitcast_fusion.2 = f32[256,256]{1,0:T(8,128)} fusion(f32[2,512,256]{2,1,0:T(8,128)S(1)} %fusion.2), kind=kOutput, calls=%fused_computation.10 | convolution fusion | flops 805306368 | bytes 1310720 | tf_op jit(solution)/shard_map/dot_general | solution.py:71
  73.6 82.6 %all-gather.3.cloned.1.call-done = f32[8192,256]{1,0:T(8,128)} async-done(((f32[256,256]{1,0:T(8,128)}), f32[8192,256]{1,0:T(8,128)}) %all-gather.3.cloned.1.call-update) | async-done | bytes 8388624 | tf_op jit(solution)/shard_map/all_gather | solution.py:10
  156.3 3.9 %reduce_sum.11 = f32[256,256]{1,0:T(8,128)S(1)} reduce(f32[32,256,256]{2,1,0:T(8,128)} %bitcast.64, f32[]{:T(128)} %constant.107.clone.1), dimensions={0}, to_apply=%region_0.1 | reduce | flops 2031616 | bytes 8650756 | tf_op jit(solution)/shard_map/reduce_sum | solution.py:11
  162.7 11.7 %cholesky.50 = f32[128,128]{1,0:T(8,128)S(1)} custom-call(f32[128,128]{1,0:T(8,128)S(1)} %cholesky.118), custom_call_target="Cholesky" | custom-call | tf_op jit(solution)/shard_map/jit(cholesky)/cholesky | solution.py:75
  174.5 9.8 %custom-call.14 = f32[1,128,128]{1,2,0:T(8,128)S(1)} custom-call(f32[1,128,128]{2,1,0:T(8,128)S(1)} %get-tuple-element.32), custom_call_target="InvertDiagBlocksLowerTriangular" | custom-call | tf_op jit(solution)/shard_map/jit(cholesky)/cholesky | solution.py:75
  184.3 1.0 constant_dynamic-update-slice_fusion.1
  185.4 1.1 convolution_subtract_fusion
  186.5 11.9 %cholesky.105 = f32[128,128]{1,0:T(8,128)S(1)} custom-call(f32[128,128]{1,0:T(8,128)S(1)} %convolution_subtract_fusion), custom_call_target="Cholesky" | custom-call | tf_op jit(solution)/shard_map/jit(cholesky)/cholesky | solution.py:75
  200.4 1.0 select_select_fusion
  201.5 5.3 %while.1 = (s32[]{:T(128)}, f32[256,256]{1,0:T(8,128)S(1)}, s32[2,2]{1,0:T(2,128)S(1)}, f32[2,128,128]{2,1,0:T(8,128)}, s32[]{:T(128)}) while((s32[]{:T(128)}, f32[256,256]{1,0:T(8,128)S(1)}, s32[2,2]{1,0:T(2,128)S(1)}, f32[2,128,128]{2,1,0:T(8,128)}, s32[]{:T(128)}) %tuple.27), condition=%wide.while_cond, body=%wide.while_body.sunk | while | flops 2 | bytes 132705 | solution.py:76
  202.1 2.0 bitcast_dynamic-update-slice_fusion.2
  204.8 2.0 bitcast_dynamic-update-slice_fusion.2
  206.7 20.5 %custom-call.15 = f32[2,128,128]{1,2,0:T(8,128)S(1)} custom-call(f32[2,128,128]{2,1,0:T(8,128)} %get-tuple-element.12), custom_call_target="InvertDiagBlocksLowerTriangular" | custom-call | tf_op jit(solution)/shard_map/triangular_solve | solution.py:76
  227.2 1.7 fusion.5
  228.9 1.0 fusion.8
  229.9 1.7 fusion.4
  231.6 1.0 pad_maximum_fusion.1
  232.6 2.5 %copy.55 = f32[1024,256]{1,0:T(8,128)} copy(f32[1024,256]{0,1:T(8,128)} %pad_maximum_fusion.1) | data formatting | bytes 2097152 | tf_op jit(solution)/shard_map/triangular_solve | solution.py:76
  (38 shorter events, 10.1 us)
Async XLA Ops:
  6.5 19.2 %copy-start = (bf16[6,512,512]{2,1,0:T(8,128)(2,1)S(1)}, bf16[6,512,512]{2,1,0:T(8,128)(2,1)}, u32[]{:S(2)}) copy-start(bf16[6,512,512]{2,1,0:T(8,128)(2,1)} %param.5) | copy-start | bytes 9437188
  6.5 149.7 %all-gather.3.cloned.1.call-start = ((), (), s32[]{:S(2)}) async-start(), calls=%async_computation | async-start | bytes 8650752 | tf_op jit(solution)/shard_map/all_gather | solution.py:10
  6.5 13.6 %collective-permute-start = (bf16[1024,256]{1,0:T(8,128)(2,1)}, bf16[1024,256]{1,0:T(8,128)(2,1)S(1)}, u32[]{:S(2)}, u32[]{:S(2)}) collective-permute-start(bf16[1024,256]{1,0:T(8,128)(2,1)} %param.9), channel_id=1, source_target_pairs={{0,1},{1,2},{2,3},{3,4},{4,5},{5,6},{6,7},{7,8},{8,9},{9,10},{10,1... | collective-permute-start | bytes 1572872 | tf_op jit(solution)/shard_map/ppermute | solution.py:20
  7.0 13.1 %collective-permute-start.1 = (bf16[1024,256]{1,0:T(8,128)(2,1)}, bf16[1024,256]{1,0:T(8,128)(2,1)S(1)}, u32[]{:S(2)}, u32[]{:S(2)}) collective-permute-start(bf16[1024,256]{1,0:T(8,128)(2,1)} %param.9), channel_id=1, source_target_pairs={{1,0},{2,1},{3,2},{4,3},{5,4},{6,5},{7,6},{8,7},{9,8},{10,9},{11,1... | collective-permute-start | bytes 1572872 | tf_op jit(solution)/shard_map/ppermute | solution.py:23
  57.5 12.4 %collective-permute-start.2 = (bf16[1024,256]{1,0:T(8,128)(2,1)S(1)}, bf16[1024,256]{1,0:T(8,128)(2,1)S(1)}, u32[]{:S(2)}, u32[]{:S(2)}) collective-permute-start(bf16[1024,256]{1,0:T(8,128)(2,1)S(1)} %bitcast.66), channel_id=1, source_target_pairs={{31,0},{0,1},{1,2},{2,3},{3,4},{4,5},{5,6},{6,7},{7,8},{8,9},{9,10... | collective-permute-start | bytes 1572872 | tf_op jit(solution)/shard_map/ppermute | solution.py:31
  61.6 8.3 %collective-permute-start.3 = (bf16[1024,256]{1,0:T(8,128)(2,1)S(1)}, bf16[1024,256]{1,0:T(8,128)(2,1)S(1)}, u32[]{:S(2)}, u32[]{:S(2)}) collective-permute-start(bf16[1024,256]{1,0:T(8,128)(2,1)S(1)} %bitcast.67), channel_id=1, source_target_pairs={{1,0},{2,1},{3,2},{4,3},{5,4},{6,5},{7,6},{8,7},{9,8},{10,9},{11,1... | collective-permute-start | bytes 1572872 | tf_op jit(solution)/shard_map/ppermute | solution.py:31
  70.0 1.0 copy-start.1
  162.0 0.7 copy-start.3
  198.4 2.0 copy-start.2
Sparse Core Ops, SparseCore 0:
  73.7 82.5 all-gather.2
